TPU v7x, 32 devices: a whole 2x2x4 slice. The times are simulated.
32 devices in a mesh: gx: 4 (over z), gy: 4 (over x, core), gz: 2 (over y).
Axes of the slice: x: 2, y: 2, z: 4, core: 2. Of those that a mesh axis runs over, the one named last changes fastest.
Arguments:
- pair: bfloat16 [1024, 1024, 128], P('gx', 'gy'), may hold values from -8 to 8, as said below
- residue_mask: int32 [1024], replicated, may hold values 0 or 1
- ln_in_gain: float32 [128], replicated, may hold values from 0.1 to 1.9
- w_proj: bfloat16 [128, 4, 128], P(None, None, 'gz'), may hold values from -0.5 to 0.5
- w_gate: bfloat16 [128, 128], replicated, may hold values from -0.5 to 0.5
- ln_out_gain: float32 [128], replicated, may hold values from 0.1 to 1.9
- w_out: bfloat16 [128, 128], replicated, may hold values from -0.5 to 0.5
Outputs:
- update: bfloat16 [128, 1024, 1024], P(None, ('gx', 'gz'), 'gy')
- energy: float32 [], replicated
Inputs may be any that keep to these rules, and one draw needn't show every extreme that they name: pair is symmetric in its two residue indices: pair[i, j, c] equals pair[j, i, c].
All inputs are finite; a program needn't handle non-finite values.
Results may differ from a plain program's by a relative error of at most 0.0083.
Values may be sent and summed in bfloat16 or wider, within the bound.
A program may use at most 256 MiB of HBM per device.

v0:
```python
import jax
import jax.numpy as jnp
from jax import lax
from jax.sharding import PartitionSpec as P

NORM_EPS = 1e-05


def layer_norm(values, gain_vec, axis):
    mean_val = jnp.mean(values, axis=axis, keepdims=True)
    centred = values - mean_val
    variance = jnp.mean(centred * centred, axis=axis, keepdims=True)
    return centred * lax.rsqrt(variance + NORM_EPS) * gain_vec


def batched(first, second):
    return jnp.einsum("hik,hkj->hij", first, second, preferred_element_type=jnp.float32)


def local(pair, residue_mask, ln_in_gain, w_proj, w_gate, ln_out_gain, w_out):
    tile_len = pair.shape[0]
    channel_count = pair.shape[2]
    grid_len = lax.axis_size("gx")
    slab_count = lax.axis_size("gz")
    slab_rows = tile_len // slab_count
    total_len = tile_len * grid_len
    row_block = lax.axis_index("gx")
    col_block = lax.axis_index("gy")
    slab_index = lax.axis_index("gz")
    mask_float = residue_mask.astype(jnp.float32)
    row_mask = lax.dynamic_slice_in_dim(mask_float, row_block * tile_len, tile_len)
    col_mask = lax.dynamic_slice_in_dim(mask_float, col_block * tile_len, tile_len)
    tile_mask = row_mask[:, None] * col_mask[None, :]
    normed = layer_norm(pair.astype(jnp.float32), ln_in_gain, -1).astype(jnp.bfloat16)
    projected = jnp.einsum("ijd,dkh->khij", normed, w_proj, preferred_element_type=jnp.float32)
    left_tile = (tile_mask * jax.nn.sigmoid(projected[0]) * projected[1]).astype(jnp.bfloat16)
    right_tile = (tile_mask * jax.nn.sigmoid(projected[2]) * projected[3]).astype(jnp.bfloat16)
    col_left, col_right = (
        lax.all_gather(left_tile, "gx", axis=1, tiled=True),
        lax.all_gather(right_tile, "gx", axis=1, tiled=True),
    )
    piece_left = lax.all_gather(left_tile, "gy", axis=2, tiled=True)
    piece_right = lax.all_gather(right_tile, "gy", axis=2, tiled=True)
    below_left = col_left
    below_right = col_right
    below_left, below_right = (below_left, below_right)
    summed = batched(piece_left, below_right) + batched(piece_right, below_left)
    tri_map = (0.5 * summed).astype(jnp.bfloat16)
    tri_normed = layer_norm(
        lax.all_to_all(tri_map, "gz", split_axis=1, concat_axis=0, tiled=True).astype(jnp.float32),
        ln_out_gain[:, None, None],
        0,
    ).astype(jnp.bfloat16)
    mixed = jnp.einsum("hij,hc->cij", tri_normed, w_out, preferred_element_type=jnp.float32)
    slab_normed = lax.dynamic_slice_in_dim(normed, slab_index * slab_rows, slab_rows, 0)
    gate_vals = jax.nn.sigmoid(
        jnp.einsum("ijd,dc->cij", slab_normed, w_gate, preferred_element_type=jnp.float32)
    )
    update = (gate_vals * mixed).astype(jnp.bfloat16)
    row_start = row_block * tile_len + slab_index * slab_rows
    row_float = (row_start + jnp.arange(slab_rows, dtype=jnp.int32)).astype(jnp.float32)
    col_float = (col_block * tile_len + jnp.arange(tile_len, dtype=jnp.int32)).astype(jnp.float32)
    slab_mask = lax.dynamic_slice_in_dim(mask_float, row_start, slab_rows)
    weighting = (
        (1.0 + (row_float[:, None] + col_float[None, :]) / total_len)
        * slab_mask[:, None]
        * col_mask[None, :]
    )
    update_float = update.astype(jnp.float32)
    partial_sum = jnp.sum(update_float * update_float * weighting[None])
    energy = lax.psum(partial_sum, ("gx", "gy", "gz")) / (total_len * total_len * channel_count)
    return (update, energy)


def solution(mesh):
    in_specs = (P("gx", "gy", None), P(), P(), P(None, None, "gz"), P(), P(), P())
    out_specs = (P(None, ("gx", "gz"), "gy"), P())
    return jax.shard_map(local, mesh=mesh, in_specs=in_specs, out_specs=out_specs, check_vma=False)
```

profile of v0, /device:TPU:12, one launch (start us, length us, event | category | flops | bytes accessed | tf_op | source)
XLA Modules:
  0.0 1946.3 jit_solution(17689445060744639698)
XLA Ops:
  7.2 0.8 convert_element_type.61
  8.1 11.7 convert_reduce_fusion
  19.8 19.0 fusion.2
  39.0 0.6 copy-done.4
  39.6 0.1 broadcast_multiply_fusion
  39.7 21.9 %fusion.4 = bf16[256,256,128]{2,1,0:T(8,128)(2,1)} fusion(bf16[256,256,128]{2,1,0:T(8,128)(2,1)} %param.7, f32[128]{0:T(128)S(1)} %copy-done.7, f32[256,256]{1,0:T(8,128)S(1)} %add_rsqrt_fusion, f32[256,256]{1,0:T(8,128)S(1)} %broadcast_multiply_fusion.1), kind=kLoop, calls=%fused_computation.6 | loop fusion | flops 41943040 | bytes 34079232 | tf_op jit(solution)/shard_map/convert_element_type | solution.py:34
  61.6 35.2 %convolution_bitcast_fusion = f32[4,64,256,256]{3,1,0,2:T(8,128)} fusion(bf16[256,256,128]{2,1,0:T(8,128)(2,1)} %fusion.4, bf16[128,4,64]{0,2,1:T(8,128)(2,1)S(1)} %copy-done), kind=kOutput, calls=%fused_computation.13 | convolution fusion | flops 4294967296 | bytes 83951616 | tf_op jit(solution)/shard_map/ijd,dkh->khij/dot_general | solution.py:35
  96.8 29.8 %fusion.12 = (bf16[64,256,256]{2,0,1:T(8,128)(2,1)}, bf16[64,256,256]{2,0,1:T(8,128)(2,1)}) fusion(f32[4,64,256,256]{3,1,0,2:T(8,128)} %convolution_bitcast_fusion, f32[256,256]{1,0:T(8,128)S(1)} %broadcast_multiply_fusion), kind=kLoop, calls=%fused_computation.16 | loop fusion | flops 50331648 | bytes 84148224 | tf_op jit(solution)/shard_map/convert_element_type | solution.py:37
  126.7 0.7 all-gather.9.cloned.1.call-update
  127.5 0.7 all-gather.5.cloned.1.call-update
  128.2 0.2 all-gather.7.cloned.1.call-start
  128.4 0.3 all-gather.7.cloned.1.call-update
  128.7 557.8 %all-gather.11.cloned.1.call-done = bf16[64,1024,256]{2,0,1:T(8,128)(2,1)} async-done(((bf16[64,256,256]{2,0,1:T(8,128)(2,1)}), bf16[64,1024,256]{2,0,1:T(8,128)(2,1)}) %all-gather.11.cloned.1.call-update) | async-done | bytes 33554448 | tf_op jit(solution)/shard_map/all_gather | solution.py:39
  686.6 209.1 %all-gather.9.cloned.1.call-done = bf16[64,256,1024]{2,0,1:T(8,128)(2,1)} async-done(((bf16[64,256,256]{2,0,1:T(8,128)(2,1)}), bf16[64,256,1024]{2,0,1:T(8,128)(2,1)}) %all-gather.9.cloned.1.call-update) | async-done | bytes 33554448 | tf_op jit(solution)/shard_map/all_gather | solution.py:43
  895.7 51.4 %fusion.5 = f32[64,256,256]{2,1,0:T(8,128)} fusion(bf16[64,1024,256]{2,0,1:T(8,128)(2,1)} %all-gather.11.cloned.1.call-done, bf16[64,256,1024]{2,0,1:T(8,128)(2,1)} %all-gather.9.cloned.1.call-done), kind=kOutput, calls=%fused_computation.7 | convolution fusion | flops 8589934592 | bytes 83886080 | tf_op jit(solution)/shard_map/hik,hkj->hij/dot_general | solution.py:17
  947.0 156.2 %all-gather.5.cloned.1.call-done = bf16[64,256,1024]{2,0,1:T(8,128)(2,1)} async-done(((bf16[64,256,256]{2,0,1:T(8,128)(2,1)}), bf16[64,256,1024]{2,0,1:T(8,128)(2,1)}) %all-gather.5.cloned.1.call-update) | async-done | bytes 33554448 | tf_op jit(solution)/shard_map/all_gather | solution.py:42
  1103.3 560.7 %all-gather.7.cloned.1.call-done = bf16[64,1024,256]{2,0,1:T(8,128)(2,1)} async-done(((bf16[64,256,256]{2,0,1:T(8,128)(2,1)}), bf16[64,1024,256]{2,0,1:T(8,128)(2,1)}) %all-gather.7.cloned.1.call-update) | async-done | bytes 33554448 | tf_op jit(solution)/shard_map/all_gather | solution.py:40
  1663.9 64.8 %multiply_convert_fusion.1 = bf16[64,256,256]{2,1,0:T(8,128)(2,1)} fusion(f32[64,256,256]{2,1,0:T(8,128)} %fusion.5, bf16[64,1024,256]{2,0,1:T(8,128)(2,1)} %all-gather.7.cloned.1.call-done, bf16[64,256,1024]{2,0,1:T(8,128)(2,1)} %all-gather.5.cloned.1.call-done), kind=kOutput, calls=%fused_computation.43 | convolution fusion | flops 8602517504 | bytes 92274688 | tf_op jit(solution)/shard_map/hik,hkj->hij/dot_general | solution.py:17
  1728.7 11.4 copy.45
  1740.1 7.4 all-to-all-start
  1747.5 0.7 dynamic_slice.15
  1748.3 0.1 multiply_multiply_fusion
  1748.4 11.5 fusion.37
  1759.9 78.6 %all-to-all-done = bf16[64,256,256]{2,0,1:T(8,128)(2,1)} async-done(((bf16[64,256,256]{2,0,1:T(8,128)(2,1)}), bf16[64,256,256]{2,0,1:T(8,128)(2,1)}, u32[]{:S(2)}, u32[]{:S(2)}) %all-to-all-start) | async-done | bytes 8388640 | tf_op jit(solution)/shard_map/all_to_all | solution.py:50
  1838.5 11.5 fusion.46
  1850.0 1.2 fusion.35
  1851.2 2.2 multiply_reduce_fusion.1
  1853.5 7.7 copy.47
  1861.2 5.6 fusion.30
  1866.9 14.6 multiply_reduce_fusion
  1881.4 12.7 copy.49
  1894.2 43.7 %psum.7 = f32[]{:T(128)} all-reduce(f32[]{:T(128)} %get-tuple-element.16), channel_id=1, replica_groups=mesh['gx'=4,'gy'=4,'gz'=2] {'gx','gy','gz'}, use_global_device_ids=true, to_apply=%region_5.0 | all-reduce | flops 1 | bytes 8 | tf_op jit(solution)/shard_map/psum | solution.py:71
  (39 shorter events, 0.4 us)
Async XLA Ops:
  7.2 54.5 %copy-start = (bf16[128,4,64]{0,2,1:T(8,128)(2,1)S(1)}, bf16[128,4,64]{0,2,1:T(8,128)(2,1)}, u32[]{:S(2)}) copy-start(bf16[128,4,64]{0,2,1:T(8,128)(2,1)} %param.10) | copy-start | bytes 196612
  7.2 679.4 %all-gather.11.cloned.1.call-start = ((), (), s32[]{:S(2)}) async-start(), calls=%async_computation.4 | async-start | bytes 41943040 | tf_op jit(solution)/shard_map/all_gather | solution.py:39
  7.2 12.6 copy-start.2
  8.1 30.8 %copy-start.6 = (f32[1024]{0:T(1024)}, f32[1024]{0:T(1024)S(1)}, u32[]{:S(2)}) copy-start(f32[1024]{0:T(1024)S(1)} %convert_element_type.61) | copy-start | bytes 12292
  8.1 31.6 %copy-start.7 = (f32[128]{0:T(128)S(1)}, f32[128]{0:T(128)}, u32[]{:S(2)}) copy-start(f32[128]{0:T(128)} %param.9) | copy-start | bytes 1540
  39.0 0.6 copy-start.4
  126.7 769.0 %all-gather.9.cloned.1.call-start = ((), (), s32[]{:S(2)}) async-start(), calls=%async_computation.3 | async-start | bytes 41943040 | tf_op jit(solution)/shard_map/all_gather | solution.py:43
  127.4 975.8 %all-gather.5.cloned.1.call-start = ((), (), s32[]{:S(2)}) async-start(), calls=%async_computation.1 | async-start | bytes 41943040 | tf_op jit(solution)/shard_map/all_gather | solution.py:42
  128.2 1535.8 %all-gather.7.cloned.1.call-start = ((), (), s32[]{:S(2)}) async-start(), calls=%async_computation.2 | async-start | bytes 41943040 | tf_op jit(solution)/shard_map/all_gather | solution.py:40
  1728.7 19.6 %copy-start.5 = (f32[256]{0:T(256)S(1)}, f32[256]{0:T(256)}, u32[]{:S(2)}) copy-start(f32[256]{0:T(256)} %copy-done.4) | copy-start | bytes 3076
  1728.7 19.7 %copy-start.3 = (bf16[128,128]{1,0:T(8,128)(2,1)S(1)}, bf16[128,128]{1,0:T(8,128)(2,1)}, u32[]{:S(2)}) copy-start(bf16[128,128]{1,0:T(8,128)(2,1)} %param.11) | copy-start | bytes 98308
  1740.1 98.3 %all-to-all-start = ((bf16[64,256,256]{2,0,1:T(8,128)(2,1)}), bf16[64,256,256]{2,0,1:T(8,128)(2,1)}, u32[]{:S(2)}, u32[]{:S(2)}) async-start(bf16[64,256,256]{2,0,1:T(8,128)(2,1)} %copy.45), calls=%async_computation | async-start | bytes 16777216 | tf_op jit(solution)/shard_map/all_to_all | solution.py:50
  1853.4 7.8 copy-start.8
  1853.4 13.4 slice-start
  1853.5 13.4 slice-start.1
  1853.5 13.4 slice-start.2
  1861.2 5.6 slice-start.3
  1861.2 5.6 copy-start.9
  1866.9 71.6 %copy-start.1 = (bf16[128,4,64]{0,2,1:T(8,128)(2,1)S(1)}, bf16[128,4,64]{0,2,1:T(8,128)(2,1)}, u32[]{:S(2)}) copy-start(bf16[128,4,64]{0,2,1:T(8,128)(2,1)} %param.10) | copy-start | bytes 196612
Sparse Core Ops, SparseCore 0:
  126.8 559.7 all-gather.10
  688.7 206.9 all-gather.8
  897.2 205.9 all-gather.4
  1105.2 558.6 all-gather.6
where the time goes:
time: 1950 us
  waiting for transfers between devices  1560 us (80%)
  matrix products  177 us (9%)
  other arithmetic  104 us (5%)
  blocking collectives  43.7 us (2%)
  local copies, waits for them, and re-layouts  33.3 us (2%)
    all_gather x1, waiting for transfers between devices, local(): lax.all_gather(right_tile, 'gx', axis=1, tiled=True)  561 us
    all_gather x1, waiting for transfers between devices, local(): lax.all_gather(left_tile, 'gx', axis=1, tiled=True)  558 us
    all_gather x1, waiting for transfers between devices, local(): piece_right = lax.all_gather(right_tile, 'gy', axis=2, tiled=True)  209 us
    all_gather x1, waiting for transfers between devices, local(): piece_left = lax.all_gather(left_tile, 'gy', axis=2, tiled=True)  156 us
    dot_general x2, matrix products, batched(): jnp.einsum('hik,hkj->hij', first, second, preferred_element_type=jnp.floa...  116 us
    all_to_all x1, waiting for transfers between devices, local(): lax.all_to_all(tri_map, 'gz', split_axis=1, concat_axis=0, tiled=True)  78.6 us
    psum x1, blocking collectives, local(): lax.psum(partial_sum, ('gx', 'gy', 'gz'))  43.7 us
  transfers between devices with their start and end apart: 5, of which 5 were waited for; matrix products, arithmetic and copies ran while one was open for 3% of the time, Pallas kernels for 0%

commit v1 on v0

--- a/solution.py
+++ b/solution.py
@@ -35,22 +35,30 @@
     projected = jnp.einsum("ijd,dkh->khij", normed, w_proj, preferred_element_type=jnp.float32)
     left_tile = (tile_mask * jax.nn.sigmoid(projected[0]) * projected[1]).astype(jnp.bfloat16)
     right_tile = (tile_mask * jax.nn.sigmoid(projected[2]) * projected[3]).astype(jnp.bfloat16)
-    col_left, col_right = (
-        lax.all_gather(left_tile, "gx", axis=1, tiled=True),
-        lax.all_gather(right_tile, "gx", axis=1, tiled=True),
-    )
-    piece_left = lax.all_gather(left_tile, "gy", axis=2, tiled=True)
-    piece_right = lax.all_gather(right_tile, "gy", axis=2, tiled=True)
-    below_left = col_left
-    below_right = col_right
-    below_left, below_right = (below_left, below_right)
-    summed = batched(piece_left, below_right) + batched(piece_right, below_left)
+    col_len = pair.shape[1]
+    col_count = lax.axis_size("gy")
+    own_count = left_tile.shape[0] // (grid_len * col_count)
+
+    def whole(tile):
+        spread = lax.all_to_all(tile, ("gx", "gy"), split_axis=0, concat_axis=0, tiled=True)
+        spread = spread.reshape(grid_len, col_count, own_count, tile_len, col_len)
+        return spread.transpose(2, 0, 3, 1, 4).reshape(own_count, total_len, total_len)
+
+    left = whole(left_tile)
+    right = whole(right_tile)
+    summed = batched(left, right) + batched(right, left)
     tri_map = (0.5 * summed).astype(jnp.bfloat16)
-    tri_normed = layer_norm(
-        lax.all_to_all(tri_map, "gz", split_axis=1, concat_axis=0, tiled=True).astype(jnp.float32),
-        ln_out_gain[:, None, None],
-        0,
-    ).astype(jnp.bfloat16)
+    outgoing = tri_map.reshape(own_count, grid_len, slab_count, slab_rows, col_count, col_len)
+    outgoing = outgoing.transpose(1, 4, 2, 0, 3, 5).reshape(-1, slab_rows, col_len)
+    arrived = lax.all_to_all(outgoing, ("gx", "gy", "gz"), split_axis=0, concat_axis=0, tiled=True)
+
+    def by_arrival(table):
+        parts = table.reshape((slab_count, grid_len, col_count, own_count) + table.shape[1:])
+        return jnp.moveaxis(parts, 0, 2).reshape(table.shape)
+
+    ln_out_gain = by_arrival(ln_out_gain)
+    w_out = by_arrival(w_out)
+    tri_normed = layer_norm(arrived.astype(jnp.float32), ln_out_gain[:, None, None], 0).astype(jnp.bfloat16)
     mixed = jnp.einsum("hij,hc->cij", tri_normed, w_out, preferred_element_type=jnp.float32)
     slab_normed = lax.dynamic_slice_in_dim(normed, slab_index * slab_rows, slab_rows, 0)
     gate_vals = jax.nn.sigmoid(

time: 1950 us -> 887 us (0.45)
  waiting for transfers between devices: 1560 us -> 494 us
  local copies, waits for them, and re-layouts: 33.3 us -> 111 us
  matrix products: 177 us -> 101 us
    all_gather x4 -> x0, waiting for transfers between devices: 1480 us -> none  [the longest x1 561 us: local(): lax.all_gather(right_tile, 'gx', axis=1, tiled=True)]
    all_to_all x1 -> x3, waiting for transfers between devices: 78.6 us -> 494 us  [the longest x2 324 us: whole(): lax.all_to_all(tile, ('gx', 'gy'), split_axis=0, concat_axis=0, tiled=True)]
    dot_general x2, matrix products: 116 us -> 35 us  [batched(): jnp.einsum('hik,hkj->hij', first, second, preferred_element_type=jnp.floa...]
    reshape x0 -> x7, local copies, waits for them, and re-layouts: none -> 73.8 us  [the longest x2 28.6 us: whole(): spread.transpose(2, 0, 3, 1, 4).reshape(own_count, total_len, total_len)]
  transfers between devices with their start and end apart: 5 -> 3, of which waited for: 5 -> 3; matrix products, arithmetic and copies ran while one was open for 3% -> 6% of each run, Pallas kernels for 0% -> 0%
where the time goes in v1:
time: 887 us; the launch traced here: 879 us
  waiting for transfers between devices  494 us (56%)
  local copies, waits for them, and re-layouts  111 us (13%)
  other arithmetic  105 us (12%)
  matrix products  101 us (11%)
  blocking collectives  45.9 us (5%)
  starting transfers between devices  19.3 us (2%)
    all_to_all x2, waiting for transfers between devices, whole(): lax.all_to_all(tile, ('gx', 'gy'), split_axis=0, concat_axis=0, tiled=True)  324 us
    all_to_all x1, waiting for transfers between devices, local(): lax.all_to_all(outgoing, ('gx', 'gy', 'gz'), split_axis=0, concat_axis=0,...  169 us
    psum x1, blocking collectives, local(): lax.psum(partial_sum, ('gx', 'gy', 'gz'))  45.9 us
    dot_general x1, matrix products, local(): jnp.einsum('ijd,dkh->khij', normed, w_proj, preferred_element_type=jnp.fl...  35.4 us
    dot_general x2, matrix products, batched(): jnp.einsum('hik,hkj->hij', first, second, preferred_element_type=jnp.floa...  35 us
    convert_element_type x1, other arithmetic, local(): (tile_mask * jax.nn.sigmoid(projected[2]) * projected[3]).astype(jnp.bflo...  30.2 us
    reshape x2, local copies, waits for them, and re-layouts, whole(): spread.transpose(2, 0, 3, 1, 4).reshape(own_count, total_len, total_len)  28.6 us
    reduce_sum x2, other arithmetic, layer_norm(): variance = jnp.mean(centred * centred, axis=axis, keepdims=True)  24.6 us
  transfers between devices with their start and end apart: 3, of which 3 were waited for; matrix products, arithmetic and copies ran while one was open for 6% of the time, Pallas kernels for 0%

profile of v1, /device:TPU:12, one launch (start us, length us, event | category | flops | bytes accessed | tf_op | source)
XLA Modules:
  0.0 878.7 jit_solution(4501811747853597107)
XLA Ops:
  0.7 0.8 convert_element_type.46
  1.5 11.7 %convert_reduce_fusion = f32[256,256]{1,0:T(8,128)S(1)} fusion(bf16[256,256,128]{2,1,0:T(8,128)(2,1)} %param.7), kind=kLoop, calls=%fused_computation.1 | loop fusion | flops 16711680 | bytes 17039360 | tf_op jit(solution)/shard_map/reduce_sum | solution.py:10
  13.3 19.0 %fusion.2 = f32[256,256]{1,0:T(8,128)S(1)} fusion(bf16[256,256,128]{2,1,0:T(8,128)(2,1)S(1)} %copy-done.2, f32[256,256]{1,0:T(8,128)S(1)} %broadcast_multiply_fusion.1), kind=kLoop, calls=%fused_computation.4 | loop fusion | flops 33488896 | bytes 17301504 | tf_op jit(solution)/shard_map/reduce_sum | solution.py:12
  32.4 0.5 copy-done.5
  33.1 21.9 %fusion.4 = bf16[256,256,128]{2,1,0:T(8,128)(2,1)} fusion(bf16[256,256,128]{2,1,0:T(8,128)(2,1)} %param.7, f32[128]{0:T(128)S(1)} %copy-done.8, f32[256,256]{1,0:T(8,128)S(1)} %add_rsqrt_fusion, f32[256,256]{1,0:T(8,128)S(1)} %broadcast_multiply_fusion.1), kind=kLoop, calls=%fused_computation.6 | loop fusion | flops 41943040 | bytes 34079232 | tf_op jit(solution)/shard_map/convert_element_type | solution.py:34
  55.0 35.4 %convolution_bitcast_fusion = f32[4,64,256,256]{3,1,0,2:T(8,128)} fusion(bf16[256,256,128]{2,1,0:T(8,128)(2,1)} %fusion.4, bf16[128,4,64]{0,2,1:T(8,128)(2,1)S(1)} %copy-done), kind=kOutput, calls=%fused_computation.7 | convolution fusion | flops 4294967296 | bytes 83951616 | tf_op jit(solution)/shard_map/ijd,dkh->khij/dot_general | solution.py:35
  90.4 30.2 %fusion.11 = (bf16[64,256,256]{2,0,1:T(8,128)(2,1)}, bf16[64,256,256]{2,0,1:T(8,128)(2,1)}) fusion(f32[4,64,256,256]{3,1,0,2:T(8,128)} %convolution_bitcast_fusion, f32[256,256]{1,0:T(8,128)S(1)} %broadcast_multiply_fusion), kind=kLoop, calls=%fused_computation.17 | loop fusion | flops 50331648 | bytes 84148224 | tf_op jit(solution)/shard_map/convert_element_type | solution.py:37
  120.6 11.4 %copy.30 = bf16[64,256,256]{2,1,0:T(8,128)(2,1)} copy(bf16[64,256,256]{2,0,1:T(8,128)(2,1)} %get-tuple-element.9) | data formatting | bytes 16777216 | tf_op jit(solution)/shard_map/convert_element_type | solution.py:36
  131.9 6.3 all-to-all-start
  138.2 11.4 %copy.33 = bf16[64,256,256]{2,1,0:T(8,128)(2,1)} copy(bf16[64,256,256]{2,0,1:T(8,128)(2,1)} %get-tuple-element.8) | data formatting | bytes 16777216 | tf_op jit(solution)/shard_map/convert_element_type | solution.py:37
  149.5 169.3 %all-to-all-done = bf16[64,256,256]{2,1,0:T(8,128)(2,1)} async-done(((bf16[64,256,256]{2,1,0:T(8,128)(2,1)}), bf16[64,256,256]{2,1,0:T(8,128)(2,1)}, u32[]{:S(2)}, u32[]{:S(2)}) %all-to-all-start) | async-done | bytes 8388640 | tf_op jit(solution)/shard_map/all_to_all | solution.py:43
  318.9 6.8 all-to-all-start.1
  325.6 11.1 %copy.53 = bf16[4,4,4,256,256]{4,1,3,0,2:T(4,128)(2,1)} copy(bf16[4,4,4,256,256]{4,3,2,1,0:T(8,128)(2,1)} %bitcast.7) | data formatting | bytes 16777216 | tf_op jit(solution)/shard_map/reshape | solution.py:44
  336.7 14.3 %reshape.162 = bf16[4,1024,1024]{2,1,0:T(8,128)(2,1)} reshape(bf16[4,4,256,4,256]{4,3,2,1,0:T(4,128)(2,1)} %bitcast.97) | data formatting | bytes 16777216 | tf_op jit(solution)/shard_map/reshape | solution.py:45
  351.0 155.1 %all-to-all-done.1 = bf16[64,256,256]{2,1,0:T(8,128)(2,1)} async-done(((bf16[64,256,256]{2,1,0:T(8,128)(2,1)}), bf16[64,256,256]{2,1,0:T(8,128)(2,1)}, u32[]{:S(2)}, u32[]{:S(2)}) %all-to-all-start.1) | async-done | bytes 8388640 | tf_op jit(solution)/shard_map/all_to_all | solution.py:43
  506.1 11.1 %copy.52 = bf16[4,4,4,256,256]{4,1,3,0,2:T(4,128)(2,1)} copy(bf16[4,4,4,256,256]{4,3,2,1,0:T(8,128)(2,1)} %bitcast.11) | data formatting | bytes 16777216 | tf_op jit(solution)/shard_map/reshape | solution.py:44
  517.2 14.4 %reshape.164 = bf16[4,1024,1024]{2,1,0:T(8,128)(2,1)} reshape(bf16[4,4,256,4,256]{4,3,2,1,0:T(4,128)(2,1)} %bitcast.98) | data formatting | bytes 16777216 | tf_op jit(solution)/shard_map/reshape | solution.py:45
  531.6 16.9 %fusion.37 = f32[4,1024,1024]{2,1,0:T(8,128)} fusion(bf16[4,1024,1024]{2,1,0:T(8,128)(2,1)} %reshape.162, bf16[4,1024,1024]{2,1,0:T(8,128)(2,1)} %reshape.164), kind=kOutput, calls=%fused_computation.57 | convolution fusion | flops 8589934592 | bytes 33554432 | tf_op jit(solution)/shard_map/hik,hkj->hij/dot_general | solution.py:17
  548.5 18.1 %multiply_convert_fusion.1 = bf16[4,1024,1024]{2,1,0:T(8,128)(2,1)} fusion(f32[4,1024,1024]{2,1,0:T(8,128)} %fusion.37, bf16[4,1024,1024]{2,1,0:T(8,128)(2,1)} %reshape.164, bf16[4,1024,1024]{2,1,0:T(8,128)(2,1)} %reshape.162), kind=kOutput, calls=%fused_computation.38 | convolution fusion | flops 8602517504 | bytes 41943040 | tf_op jit(solution)/shard_map/hik,hkj->hij/dot_general | solution.py:17
  566.6 14.5 %reshape.165 = bf16[4,4,2,128,4,256]{5,4,3,2,1,0:T(4,128)(2,1)} reshape(bf16[4,1024,1024]{2,1,0:T(8,128)(2,1)} %multiply_convert_fusion.1) | data formatting | bytes 16777216 | tf_op jit(solution)/shard_map/reshape | solution.py:51
  581.1 8.4 copy.35
  589.5 6.2 all-to-all-start.2
  595.9 0.1 mul.154
  596.1 0.8 dynamic_slice.15
  597.0 11.4 %fusion.28 = f32[128,256,128]{2,1,0:T(8,128)} fusion(bf16[256,256,128]{2,1,0:T(8,128)(2,1)} %fusion.4, s32[]{:T(128)S(6)} %select_n.12, bf16[128,128]{1,0:T(8,128)(2,1)S(1)} %copy-done.3), kind=kOutput, calls=%fused_computation.42 | convolution fusion | flops 1073741824 | bytes 25198596 | tf_op jit(solution)/shard_map/ijd,dc->cij/dot_general | solution.py:65
  608.4 169.2 %all-to-all-done.2 = bf16[128,128,256]{2,1,0:T(8,128)(2,1)} async-done(((bf16[128,128,256]{2,1,0:T(8,128)(2,1)}), bf16[128,128,256]{2,1,0:T(8,128)(2,1)}, u32[]{:S(2)}, u32[]{:S(2)}) %all-to-all-start.2) | async-done | bytes 8388640 | tf_op jit(solution)/shard_map/all_to_all | solution.py:53
  777.6 4.6 convert_reduce_fusion.1
  782.2 5.6 fusion.7
  787.8 10.8 %fusion.9 = bf16[128,128,256]{2,1,0:T(8,128)(2,1)} fusion(bf16[128,128,256]{2,1,0:T(8,128)(2,1)} %all-to-all-done.2, f32[128]{0:T(128)S(1)} %mul.154, f32[128,256]{1,0:T(8,128)S(1)} %add_rsqrt_fusion.1, f32[128,256]{1,0:T(8,128)S(1)} %broadcast_multiply_fusion.2), kind=kLoop, calls=%fused_computation.14 | loop fusion | flops 20971520 | bytes 17039872 | tf_op jit(solution)/shard_map/convert_element_type | solution.py:61
  798.6 19.4 %multiply_reduce_fusion = (f32[]{:T(128)}, bf16[128,128,256]{0,2,1:T(8,128)(2,1)}) fusion(f32[128,256]{1,0:T(8,128)S(1)} %multiply_multiply_fusion, bf16[128,128,1]{1,0,2:T(8,128)(2,1)S(1)} %bitcast.101, bf16[128,128,256]{2,1,0:T(8,128)(2,1)} %fusion.9, f32[128,256,128]{2,1,0:T(8,128)} %fusion.28), kind=kOutput, calls=%fused_computation.37 | convolution fusion | flops 1111490560 | bytes 33718276 | tf_op jit(solution)/shard_map/hij,hc->cij/dot_general | solution.py:62
  818.0 12.7 %copy.39 = bf16[128,128,256]{2,1,0:T(8,128)(2,1)} copy(bf16[128,128,256]{0,2,1:T(8,128)(2,1)} %get-tuple-element.13) | data formatting | bytes 16777216
  830.8 45.9 %psum.7 = f32[]{:T(128)} all-reduce(f32[]{:T(128)} %get-tuple-element.12), channel_id=1, replica_groups=mesh['gx'=4,'gy'=4,'gz'=2] {'gx','gy','gz'}, use_global_device_ids=true, to_apply=%region_5.0 | all-reduce | flops 1 | bytes 8 | tf_op jit(solution)/shard_map/psum | solution.py:79
  (31 shorter events, 0.6 us)
Async XLA Ops:
  0.6 54.4 %copy-start = (bf16[128,4,64]{0,2,1:T(8,128)(2,1)S(1)}, bf16[128,4,64]{0,2,1:T(8,128)(2,1)}, u32[]{:S(2)}) copy-start(bf16[128,4,64]{0,2,1:T(8,128)(2,1)} %param.10) | copy-start | bytes 196612
  0.7 12.6 %copy-start.2 = (bf16[256,256,128]{2,1,0:T(8,128)(2,1)S(1)}, bf16[256,256,128]{2,1,0:T(8,128)(2,1)}, u32[]{:S(2)}) copy-start(bf16[256,256,128]{2,1,0:T(8,128)(2,1)} %param.7) | copy-start | bytes 50331652
  1.5 30.8 %copy-start.7 = (f32[1024]{0:T(1024)}, f32[1024]{0:T(1024)S(1)}, u32[]{:S(2)}) copy-start(f32[1024]{0:T(1024)S(1)} %convert_element_type.46) | copy-start | bytes 12292
  1.5 31.5 %copy-start.8 = (f32[128]{0:T(128)S(1)}, f32[128]{0:T(128)}, u32[]{:S(2)}) copy-start(f32[128]{0:T(128)} %param.9) | copy-start | bytes 1540
  32.4 0.5 copy-start.5
  131.9 186.9 %all-to-all-start = ((bf16[64,256,256]{2,1,0:T(8,128)(2,1)}), bf16[64,256,256]{2,1,0:T(8,128)(2,1)}, u32[]{:S(2)}, u32[]{:S(2)}) async-start(bf16[64,256,256]{2,1,0:T(8,128)(2,1)} %copy.30), calls=%async_computation | async-start | bytes 16777216 | tf_op jit(solution)/shard_map/all_to_all | solution.py:43
  318.9 187.3 %all-to-all-start.1 = ((bf16[64,256,256]{2,1,0:T(8,128)(2,1)}), bf16[64,256,256]{2,1,0:T(8,128)(2,1)}, u32[]{:S(2)}, u32[]{:S(2)}) async-start(bf16[64,256,256]{2,1,0:T(8,128)(2,1)} %copy.33), calls=%async_computation.1 | async-start | bytes 16777216 | tf_op jit(solution)/shard_map/all_to_all | solution.py:43
  581.1 14.7 %copy-start.9 = (f32[128]{0:T(128)S(1)}, f32[128]{0:T(128)}, u32[]{:S(2)}) copy-start(f32[128]{0:T(128)} %param.12) | copy-start | bytes 1540
  581.1 15.7 %copy-start.4 = (bf16[128,128]{1,0:T(8,128)(2,1)S(1)}, bf16[128,128]{1,0:T(8,128)(2,1)}, u32[]{:S(2)}) copy-start(bf16[128,128]{1,0:T(8,128)(2,1)} %param.13) | copy-start | bytes 98308
  581.1 15.8 %copy-start.6 = (f32[256]{0:T(256)S(1)}, f32[256]{0:T(256)}, u32[]{:S(2)}) copy-start(f32[256]{0:T(256)} %copy-done.5) | copy-start | bytes 3076
  581.1 15.9 %copy-start.3 = (bf16[128,128]{1,0:T(8,128)(2,1)S(1)}, bf16[128,128]{1,0:T(8,128)(2,1)}, u32[]{:S(2)}) copy-start(bf16[128,128]{1,0:T(8,128)(2,1)} %param.11) | copy-start | bytes 98308
  589.5 188.0 %all-to-all-start.2 = ((bf16[128,128,256]{2,1,0:T(8,128)(2,1)}), bf16[128,128,256]{2,1,0:T(8,128)(2,1)}, u32[]{:S(2)}, u32[]{:S(2)}) async-start(bf16[128,128,256]{2,1,0:T(8,128)(2,1)} %bitcast.96), calls=%async_computation.2 | async-start | bytes 16777216 | tf_op jit(solution)/shard_map/all_to_all | solution.py:53
  798.6 78.8 %copy-start.1 = (bf16[128,4,64]{0,2,1:T(8,128)(2,1)S(1)}, bf16[128,4,64]{0,2,1:T(8,128)(2,1)}, u32[]{:S(2)}) copy-start(bf16[128,4,64]{0,2,1:T(8,128)(2,1)} %param.10) | copy-start | bytes 196612

commit v2 on v1

--- a/solution.py
+++ b/solution.py
@@ -32,29 +32,39 @@
     col_mask = lax.dynamic_slice_in_dim(mask_float, col_block * tile_len, tile_len)
     tile_mask = row_mask[:, None] * col_mask[None, :]
     normed = layer_norm(pair.astype(jnp.float32), ln_in_gain, -1).astype(jnp.bfloat16)
-    projected = jnp.einsum("ijd,dkh->khij", normed, w_proj, preferred_element_type=jnp.float32)
-    left_tile = (tile_mask * jax.nn.sigmoid(projected[0]) * projected[1]).astype(jnp.bfloat16)
-    right_tile = (tile_mask * jax.nn.sigmoid(projected[2]) * projected[3]).astype(jnp.bfloat16)
     col_len = pair.shape[1]
     col_count = lax.axis_size("gy")
-    own_count = left_tile.shape[0] // (grid_len * col_count)
+    hidden_here = w_proj.shape[2]
+    own_count = hidden_here // (grid_len * col_count)
+    piece_count = 2 if own_count % 2 == 0 else 1
+    part = own_count // piece_count
+    w_parts = w_proj.reshape(channel_count, 4, grid_len * col_count, piece_count, part)
 
-    def whole(tile):
+    def operand(weights):
+        projected = jnp.einsum("ijd,dkh->khij", normed, weights, preferred_element_type=jnp.float32)
+        tile = (tile_mask * jax.nn.sigmoid(projected[0]) * projected[1]).astype(jnp.bfloat16)
         spread = lax.all_to_all(tile, ("gx", "gy"), split_axis=0, concat_axis=0, tiled=True)
-        spread = spread.reshape(grid_len, col_count, own_count, tile_len, col_len)
-        return spread.transpose(2, 0, 3, 1, 4).reshape(own_count, total_len, total_len)
+        spread = spread.reshape(grid_len, col_count, part, tile_len, col_len)
+        return spread.transpose(2, 0, 3, 1, 4).reshape(part, total_len, total_len)
 
-    left = whole(left_tile)
-    right = whole(right_tile)
-    summed = batched(left, right) + batched(right, left)
-    tri_map = (0.5 * summed).astype(jnp.bfloat16)
-    outgoing = tri_map.reshape(own_count, grid_len, slab_count, slab_rows, col_count, col_len)
-    outgoing = outgoing.transpose(1, 4, 2, 0, 3, 5).reshape(-1, slab_rows, col_len)
-    arrived = lax.all_to_all(outgoing, ("gx", "gy", "gz"), split_axis=0, concat_axis=0, tiled=True)
+    pieces = []
+    for piece in range(piece_count):
+        weights = w_parts[:, :, :, piece].reshape(channel_count, 4, -1)
+        left = operand(weights[:, :2])
+        right = operand(weights[:, 2:])
+        summed = batched(left, right) + batched(right, left)
+        tri_map = (0.5 * summed).astype(jnp.bfloat16)
+        outgoing = tri_map.reshape(part, grid_len, slab_count, slab_rows, col_count, col_len)
+        outgoing = outgoing.transpose(1, 4, 2, 0, 3, 5).reshape(-1, slab_rows, col_len)
+        pieces.append(
+            lax.all_to_all(outgoing, ("gx", "gy", "gz"), split_axis=0, concat_axis=0, tiled=True)
+        )
+    arrived = jnp.concatenate(pieces, axis=0)
 
     def by_arrival(table):
-        parts = table.reshape((slab_count, grid_len, col_count, own_count) + table.shape[1:])
-        return jnp.moveaxis(parts, 0, 2).reshape(table.shape)
+        dims = (slab_count, grid_len, col_count, piece_count, part)
+        parts = table.reshape(dims + table.shape[1:])
+        return jnp.moveaxis(parts, (3, 1, 2), (0, 1, 2)).reshape(table.shape)
 
     ln_out_gain = by_arrival(ln_out_gain)
     w_out = by_arrival(w_out)

time: 887 us -> 820 us (0.924)
  waiting for transfers between devices: 494 us -> 399 us
  starting transfers between devices: 19.3 us -> 38.6 us
  local copies, waits for them, and re-layouts: 111 us -> 124 us
  matrix products: 101 us -> 112 us
  other arithmetic: 105 us -> 95.8 us
    all_to_all x1 -> x2, waiting for transfers between devices: 169 us -> 113 us  [local(): lax.all_to_all(outgoing, ('gx', 'gy', 'gz'), split_axis=0, concat_axis=0,...]
    all_to_all x2 -> x4, waiting for transfers between devices: 324 us -> 286 us  [operand(): lax.all_to_all(tile, ('gx', 'gy'), split_axis=0, concat_axis=0, tiled=True)]
    reshape x7 -> x13, local copies, waits for them, and re-layouts: 73.8 us -> 86.9 us  [the longest x4 31 us: operand(): return spread.transpose(2, 0, 3, 1, 4).reshape(part, total_len, total_len)]
    all_to_all x2 -> x4, starting transfers between devices: 13 us -> 26 us  [operand(): lax.all_to_all(tile, ('gx', 'gy'), split_axis=0, concat_axis=0, tiled=True)]
    dot_general x1 -> x4, matrix products: 35.4 us -> 47.1 us  [operand(): jnp.einsum('ijd,dkh->khij', normed, weights, preferred_element_type=jnp.f...]
    dot_general x2 -> x4, matrix products: 35 us -> 27.4 us  [batched(): jnp.einsum('hik,hkj->hij', first, second, preferred_element_type=jnp.floa...]
    convert_element_type x2 -> x4, local copies, waits for them, and re-layouts: 22.7 us -> 24 us  [operand(): (tile_mask * jax.nn.sigmoid(projected[0]) * projected[1]).astype(jnp.bflo...]
  transfers between devices with their start and end apart: 3 -> 6, of which waited for: 3 -> 6; matrix products, arithmetic and copies ran while one was open for 6% -> 18% of each run, Pallas kernels for 0% -> 0%
where the time goes in v2:
time: 820 us; the launch traced here: 816 us
  waiting for transfers between devices  399 us (49%)
  local copies, waits for them, and re-layouts  124 us (15%)
  matrix products  112 us (14%)
  other arithmetic  95.8 us (12%)
  blocking collectives  42.7 us (5%)
  starting transfers between devices  38.6 us (5%)
    all_to_all x4, waiting for transfers between devices, operand(): lax.all_to_all(tile, ('gx', 'gy'), split_axis=0, concat_axis=0, tiled=True)  286 us
    all_to_all x2, waiting for transfers between devices, local(): lax.all_to_all(outgoing, ('gx', 'gy', 'gz'), split_axis=0, concat_axis=0,...  113 us
    dot_general x4, matrix products, operand(): jnp.einsum('ijd,dkh->khij', normed, weights, preferred_element_type=jnp.f...  47.1 us
    psum x1, blocking collectives, local(): lax.psum(partial_sum, ('gx', 'gy', 'gz'))  42.7 us
    reshape x4, local copies, waits for them, and re-layouts, operand(): return spread.transpose(2, 0, 3, 1, 4).reshape(part, total_len, total_len)  31 us
    reshape x4, local copies, waits for them, and re-layouts, operand(): spread = spread.reshape(grid_len, col_count, part, tile_len, col_len)  29.8 us
    convert_element_type x1, other arithmetic, operand(): (tile_mask * jax.nn.sigmoid(projected[0]) * projected[1]).astype(jnp.bflo...  27.8 us
    dot_general x4, matrix products, batched(): jnp.einsum('hik,hkj->hij', first, second, preferred_element_type=jnp.floa...  27.4 us
  transfers between devices with their start and end apart: 6, of which 6 were waited for; matrix products, arithmetic and copies ran while one was open for 18% of the time, Pallas kernels for 0%

profile of v2, /device:TPU:12, one launch (start us, length us, event | category | flops | bytes accessed | tf_op | source)
XLA Modules:
  0.0 815.7 jit_solution(17756717759695791521)
XLA Ops:
  0.7 10.8 %convert_reduce_fusion = f32[256,256]{1,0:T(8,128)S(1)} fusion(bf16[256,256,128]{2,1,0:T(8,128)(2,1)} %param.7), kind=kLoop, calls=%fused_computation.1 | loop fusion | flops 16711680 | bytes 17039360 | tf_op jit(solution)/shard_map/reduce_sum | solution.py:10
  11.5 19.0 %fusion.2 = f32[256,256]{1,0:T(8,128)S(1)} fusion(bf16[256,256,128]{2,1,0:T(8,128)(2,1)S(1)} %copy-done.2, f32[256,256]{1,0:T(8,128)S(1)} %broadcast_multiply_fusion.1), kind=kLoop, calls=%fused_computation.4 | loop fusion | flops 33488896 | bytes 17301504 | tf_op jit(solution)/shard_map/reduce_sum | solution.py:12
  30.7 21.1 %fusion.4 = bf16[256,256,128]{2,1,0:T(8,128)(2,1)S(1)} fusion(bf16[256,256,128]{2,1,0:T(8,128)(2,1)} %param.7, f32[128]{0:T(128)S(1)} %copy-done.10, f32[256,256]{1,0:T(8,128)S(1)} %add_rsqrt_fusion, f32[256,256]{1,0:T(8,128)S(1)} %broadcast_multiply_fusion.1), kind=kLoop, calls=%fused_computation.6 | loop fusion | flops 41943040 | bytes 34079232 | tf_op jit(solution)/shard_map/convert_element_type | solution.py:34
  51.8 11.8 %fusion.18 = f32[2,32,256,256]{3,1,0,2:T(8,128)} fusion(bf16[256,256,128]{2,1,0:T(8,128)(2,1)S(1)} %fusion.4, bf16[128,4,32]{0,2,1:T(8,128)(2,1)S(1)} %bitcast.169), kind=kOutput, calls=%fused_computation.24 | convolution fusion | flops 1073741824 | bytes 33570816 | tf_op jit(solution)/shard_map/ijd,dkh->khij/dot_general | solution.py:44
  63.6 11.7 %fusion.56 = f32[2,32,256,256]{3,1,2,0:T(8,128)} fusion(bf16[256,256,128]{2,1,0:T(8,128)(2,1)S(1)} %fusion.4, bf16[128,4,32]{0,2,1:T(8,128)(2,1)S(1)} %bitcast.170), kind=kOutput, calls=%fused_computation.69 | convolution fusion | flops 1073741824 | bytes 33570816 | tf_op jit(solution)/shard_map/ijd,dkh->khij/dot_general | solution.py:44
  75.2 11.7 %fusion.53 = f32[2,32,256,256]{3,1,2,0:T(8,128)} fusion(bf16[256,256,128]{2,1,0:T(8,128)(2,1)S(1)} %fusion.4, bf16[128,4,32]{0,2,1:T(8,128)(2,1)S(1)} %bitcast.167), kind=kOutput, calls=%fused_computation.68 | convolution fusion | flops 1073741824 | bytes 33570816 | tf_op jit(solution)/shard_map/ijd,dkh->khij/dot_general | solution.py:44
  86.9 12.0 %fusion.59 = f32[2,32,256,256]{3,1,2,0:T(8,128)} fusion(bf16[256,256,128]{2,1,0:T(8,128)(2,1)S(1)} %fusion.4, bf16[128,4,32]{0,2,1:T(8,128)(2,1)S(1)} %bitcast.168), kind=kOutput, calls=%fused_computation.70 | convolution fusion | flops 1073741824 | bytes 33570816 | tf_op jit(solution)/shard_map/ijd,dkh->khij/dot_general | solution.py:44
  99.1 27.8 %fusion.36 = (bf16[32,256,256]{2,0,1:T(8,128)(2,1)}, bf16[32,256,256]{2,0,1:T(8,128)(2,1)}, bf16[32,256,256]{2,0,1:T(8,128)(2,1)}, bf16[32,256,256]{2,0,1:T(8,128)(2,1)S(1)}) fusion(f32[2,32,256,256]{3,1,2,0:T(8,128)} %fusion.56, f32[256,256]{1,0:T(8,128)S(1)} %broadcast_multiply_fusion, f32[2,32,256,256]{3,1,2,0:T(8,128)} %fusion.59, ...), kind=kLoop, calls=%fused_computation.45 | loop fusion | flops 50331648 | bytes 84148224 | tf_op jit(solution)/shard_map/convert_element_type | solution.py:45
  144.2 84.3 %all-to-all-done = bf16[32,256,256]{2,1,0:T(8,128)(2,1)} async-done(((bf16[32,256,256]{2,1,0:T(8,128)(2,1)}), bf16[32,256,256]{2,1,0:T(8,128)(2,1)}, u32[]{:S(2)}, u32[]{:S(2)}) %all-to-all-start) | async-done | bytes 4194336 | tf_op jit(solution)/shard_map/all_to_all | solution.py:46
  234.9 6.6 copy.50
  241.5 84.2 %all-to-all-done.1 = bf16[32,256,256]{2,1,0:T(8,128)(2,1)} async-done(((bf16[32,256,256]{2,1,0:T(8,128)(2,1)}), bf16[32,256,256]{2,1,0:T(8,128)(2,1)}, u32[]{:S(2)}, u32[]{:S(2)}) %all-to-all-start.1) | async-done | bytes 4194336 | tf_op jit(solution)/shard_map/all_to_all | solution.py:46
  338.7 84.3 %all-to-all-done.3 = bf16[32,256,256]{2,1,0:T(8,128)(2,1)} async-done(((bf16[32,256,256]{2,1,0:T(8,128)(2,1)}), bf16[32,256,256]{2,1,0:T(8,128)(2,1)}, u32[]{:S(2)}, u32[]{:S(2)}) %all-to-all-start.3) | async-done | bytes 4194336 | tf_op jit(solution)/shard_map/all_to_all | solution.py:46
  422.9 6.8 all-to-all-start.4
  429.7 7.4 copy.83
  437.1 7.8 reshape.196
  444.9 7.4 copy.82
  452.4 7.7 reshape.198
  460.1 7.7 fusion.69
  473.8 8.0 reshape.199
  486.8 33.5 %all-to-all-done.4 = bf16[32,256,256]{2,1,0:T(8,128)(2,1)} async-done(((bf16[32,256,256]{2,1,0:T(8,128)(2,1)}), bf16[32,256,256]{2,1,0:T(8,128)(2,1)}, u32[]{:S(2)}, u32[]{:S(2)}) %all-to-all-start.4) | async-done | bytes 4194336 | tf_op jit(solution)/shard_map/all_to_all | solution.py:46
  526.6 7.4 copy.81
  534.0 7.7 reshape.202
  541.7 7.4 copy.80
  549.2 7.8 reshape.204
  556.9 7.7 fusion.70
  570.7 8.1 reshape.205
  583.8 34.0 %all-to-all-done.2 = bf16[64,128,256]{2,1,0:T(8,128)(2,1)} async-done(((bf16[64,128,256]{2,1,0:T(8,128)(2,1)}), bf16[64,128,256]{2,1,0:T(8,128)(2,1)}, u32[]{:S(2)}, u32[]{:S(2)}) %all-to-all-start.2) | async-done | bytes 4194336 | tf_op jit(solution)/shard_map/all_to_all | solution.py:60
  624.8 11.4 %fusion.51 = f32[128,256,128]{2,1,0:T(8,128)} fusion(bf16[256,256,128]{2,1,0:T(8,128)(2,1)} %copy-done.1, s32[]{:T(128)S(6)} %select_n.12, bf16[128,128]{1,0:T(8,128)(2,1)S(1)} %copy-done), kind=kOutput, calls=%fused_computation.66 | convolution fusion | flops 1073741824 | bytes 25198596 | tf_op jit(solution)/shard_map/ijd,dc->cij/dot_general | solution.py:75
  636.2 79.1 %all-to-all-done.5 = bf16[64,128,256]{2,1,0:T(8,128)(2,1)} async-done(((bf16[64,128,256]{2,1,0:T(8,128)(2,1)}), bf16[64,128,256]{2,1,0:T(8,128)(2,1)}, u32[]{:S(2)}, u32[]{:S(2)}) %all-to-all-start.5) | async-done | bytes 4194336 | tf_op jit(solution)/shard_map/all_to_all | solution.py:60
  732.3 26.0 %multiply_reduce_fusion = (f32[]{:T(128)}, bf16[128,128,256]{0,2,1:T(8,128)(2,1)}) fusion(f32[128,256]{1,0:T(8,128)S(1)} %multiply_multiply_fusion, bf16[128,128,1]{1,0,2:T(8,128)(2,1)S(1)} %bitcast.174, bf16[128,128,256]{2,1,0:T(8,128)(2,1)S(1)} %fusion.9, f32[128,256,128]{2,1,0:T(8,128)S(1)} %bitcast.160), kind=kOutput, calls=%fused_computation.23 | convolution fusion | flops 1111490560 | bytes 33718276 | tf_op jit(solution)/shard_map/hij,hc->cij/dot_general | solution.py:72
  758.3 12.7 %copy.59 = bf16[128,128,256]{2,1,0:T(8,128)(2,1)} copy(bf16[128,128,256]{0,2,1:T(8,128)(2,1)} %get-tuple-element.17) | data formatting | bytes 16777216
  771.0 42.7 %psum.7 = f32[]{:T(128)} all-reduce(f32[]{:T(128)} %get-tuple-element.16), channel_id=1, replica_groups=mesh['gx'=4,'gy'=4,'gz'=2] {'gx','gy','gz'}, use_global_device_ids=true, to_apply=%region_5.0 | all-reduce | flops 1 | bytes 8 | tf_op jit(solution)/shard_map/psum | solution.py:89
  (64 shorter events, 89.0 us)
Async XLA Ops:
  0.6 624.2 %copy-start = (bf16[128,128]{1,0:T(8,128)(2,1)S(1)}, bf16[128,128]{1,0:T(8,128)(2,1)}, u32[]{:S(2)}) copy-start(bf16[128,128]{1,0:T(8,128)(2,1)} %param.11) | copy-start | bytes 98308
  0.7 10.8 %copy-start.2 = (bf16[256,256,128]{2,1,0:T(8,128)(2,1)S(1)}, bf16[256,256,128]{2,1,0:T(8,128)(2,1)}, u32[]{:S(2)}) copy-start(bf16[256,256,128]{2,1,0:T(8,128)(2,1)} %param.7) | copy-start | bytes 50331652
  11.5 19.1 %copy-start.7 = (bf16[128,4,64]{0,2,1:T(8,128)(2,1)S(1)}, bf16[128,4,64]{0,2,1:T(8,128)(2,1)}, u32[]{:S(2)}) copy-start(bf16[128,4,64]{0,2,1:T(8,128)(2,1)} %param.10) | copy-start | bytes 196612
  11.5 19.2 %copy-start.10 = (f32[128]{0:T(128)S(1)}, f32[128]{0:T(128)}, u32[]{:S(2)}) copy-start(f32[128]{0:T(128)} %param.9) | copy-start | bytes 1540
  51.8 35.1 %copy-start.1 = (bf16[256,256,128]{2,1,0:T(8,128)(2,1)}, bf16[256,256,128]{2,1,0:T(8,128)(2,1)S(1)}, u32[]{:S(2)}) copy-start(bf16[256,256,128]{2,1,0:T(8,128)(2,1)S(1)} %fusion.4) | copy-start | bytes 50331652
  86.9 12.0 %copy-start.9 = (s32[1024]{0:T(1024)S(1)}, s32[1024]{0:T(1024)}, u32[]{:S(2)}) copy-start(s32[1024]{0:T(1024)} %param.8) | copy-start | bytes 12292
  131.4 97.1 %all-to-all-start = ((bf16[32,256,256]{2,1,0:T(8,128)(2,1)}), bf16[32,256,256]{2,1,0:T(8,128)(2,1)}, u32[]{:S(2)}, u32[]{:S(2)}) async-start(bf16[32,256,256]{2,1,0:T(8,128)(2,1)} %copy.42), calls=%async_computation | async-start | bytes 8388608 | tf_op jit(solution)/shard_map/all_to_all | solution.py:46
  228.4 97.2 %all-to-all-start.1 = ((bf16[32,256,256]{2,1,0:T(8,128)(2,1)}), bf16[32,256,256]{2,1,0:T(8,128)(2,1)}, u32[]{:S(2)}, u32[]{:S(2)}) async-start(bf16[32,256,256]{2,1,0:T(8,128)(2,1)} %copy.45), calls=%async_computation.1 | async-start | bytes 8388608 | tf_op jit(solution)/shard_map/all_to_all | solution.py:46
  325.7 97.2 %all-to-all-start.3 = ((bf16[32,256,256]{2,1,0:T(8,128)(2,1)}), bf16[32,256,256]{2,1,0:T(8,128)(2,1)}, u32[]{:S(2)}, u32[]{:S(2)}) async-start(bf16[32,256,256]{2,1,0:T(8,128)(2,1)} %copy.50), calls=%async_computation.3 | async-start | bytes 8388608 | tf_op jit(solution)/shard_map/all_to_all | solution.py:46
  422.9 97.4 %all-to-all-start.4 = ((bf16[32,256,256]{2,1,0:T(8,128)(2,1)}), bf16[32,256,256]{2,1,0:T(8,128)(2,1)}, u32[]{:S(2)}, u32[]{:S(2)}) async-start(bf16[32,256,256]{2,1,0:T(8,128)(2,1)} %copy.53), calls=%async_computation.4 | async-start | bytes 8388608 | tf_op jit(solution)/shard_map/all_to_all | solution.py:46
  460.1 7.7 copy-start.3
  460.1 7.7 copy-start.5
  520.3 97.4 %all-to-all-start.2 = ((bf16[64,128,256]{2,1,0:T(8,128)(2,1)}), bf16[64,128,256]{2,1,0:T(8,128)(2,1)}, u32[]{:S(2)}, u32[]{:S(2)}) async-start(bf16[64,128,256]{2,1,0:T(8,128)(2,1)} %bitcast.162), calls=%async_computation.2 | async-start | bytes 8388608 | tf_op jit(solution)/shard_map/all_to_all | solution.py:60
  556.9 7.7 copy-start.4
  556.9 7.7 copy-start.6
  578.8 45.4 %copy-start.11 = (f32[128]{0:T(128)S(1)}, f32[128]{0:T(128)}, u32[]{:S(2)}) copy-start(f32[128]{0:T(128)} %param.12) | copy-start | bytes 1540
  578.8 45.9 %copy-start.8 = (bf16[128,128]{1,0:T(8,128)(2,1)S(1)}, bf16[128,128]{1,0:T(8,128)(2,1)}, u32[]{:S(2)}) copy-start(bf16[128,128]{1,0:T(8,128)(2,1)} %param.13) | copy-start | bytes 98308
  617.8 97.6 %all-to-all-start.5 = ((bf16[64,128,256]{2,1,0:T(8,128)(2,1)}), bf16[64,128,256]{2,1,0:T(8,128)(2,1)}, u32[]{:S(2)}, u32[]{:S(2)}) async-start(bf16[64,128,256]{2,1,0:T(8,128)(2,1)} %bitcast.161), calls=%async_computation.5 | async-start | bytes 8388608 | tf_op jit(solution)/shard_map/all_to_all | solution.py:60
  715.4 16.8 %slice-start = ((s8[16777216]{0:T(1024)(128)(4,1)}), s8[4194304]{0:T(1024)(128)(4,1)S(1)}, s32[]{:S(2)}) async-start(s8[16777216]{0:T(1024)(128)(4,1)} %bitcast.159), calls=%async_computation.6 | async-start | bytes 8388608
  720.1 12.1 %slice-start.1 = ((s8[16777216]{0:T(1024)(128)(4,1)}), s8[4194304]{0:T(1024)(128)(4,1)S(1)}, s32[]{:S(2)}) async-start(s8[16777216]{0:T(1024)(128)(4,1)} %bitcast.159), calls=%async_computation.7 | async-start | bytes 8388608
  720.2 12.1 %slice-start.2 = ((s8[16777216]{0:T(1024)(128)(4,1)}), s8[4194304]{0:T(1024)(128)(4,1)S(1)}, s32[]{:S(2)}) async-start(s8[16777216]{0:T(1024)(128)(4,1)} %bitcast.159), calls=%async_computation.8 | async-start | bytes 8388608
  726.7 5.5 slice-start.3
